TPU v7x, 32 devices: a whole 2x2x4 slice. The times are simulated.
32 devices in a mesh: ctx: 8 (over z, core), tp: 4 (over y, x).
Axes of the slice: x: 2, y: 2, z: 4, core: 2. Of those that a mesh axis runs over, the one named last changes fastest.
Arguments:
- tokens: bfloat16 [2, 4096, 8192], P(None, 'ctx', 'tp'), may hold values from -14 to 14
- norm_gain: float32 [8192], replicated, may hold values from 0.5 to 1.5
- span_order: int32 [2, 16], replicated, may hold values from 0 to 15, each once within a row
- w_query: bfloat16 [8192, 4096], P('ctx', 'tp'), may hold values from -0.10122281 to 0.10122281
- w_key: bfloat16 [8192, 1024], P('ctx', 'tp'), may hold values from -0.10122281 to 0.10122281
- value_weight: bfloat16 [8192, 1024], P('ctx', 'tp'), may hold values from -0.0625 to 0.0625
- w_out: bfloat16 [4096, 8192], P('tp', 'ctx'), may hold values from -0.75 to 0.75
Outputs:
- mixed: bfloat16 [2, 4096, 8192], P(None, 'ctx', 'tp')
Inputs may be any that keep to these rules, and one draw needn't show every extreme that they name: Each row of span_order names every one of the 2 * 8 blocks of positions once; stored block b of a sequence holds positions span_order[b] * 256 onwards, in order.
All inputs are finite; a program needn't handle non-finite values.
Results may differ from a plain program's by a relative error of at most 0.014.
Values may be sent and summed in bfloat16 or wider, within the bound.
A program may use at most 128 MiB of HBM per device.

v0:
```python
import math
import jax
import jax.numpy as jnp
from jax import lax
from jax.sharding import PartitionSpec as P

HEAD_DIM = 128
theta_base = 500000.0
norm_eps = 1e-05
masked_score = -1e30


def normalize(flat_rows, norm_gain):
    wide = flat_rows.astype(jnp.float32)
    factor = lax.rsqrt(jnp.mean(wide * wide, axis=-1, keepdims=True) + norm_eps)
    return (wide * factor * norm_gain).astype(jnp.bfloat16)


def positions_of(span_order, first, count, block_rows):
    stored = first + jnp.arange(count, dtype=jnp.int32)
    which = stored // block_rows
    slots = jnp.arange(span_order.shape[1], dtype=jnp.int32)
    picked = jnp.sum(
        jnp.where(slots[None, None, :] == which[None, :, None], span_order[:, None, :], 0), axis=2
    )
    return picked * block_rows + stored % block_rows


def apply_rotation(value_rows, token_position, head_size):
    half = head_size // 2
    freqs = jnp.exp(-(2.0 * jnp.arange(half, dtype=jnp.float32) / head_size) * math.log(theta_base))
    angle = token_position.astype(jnp.float32)[..., None] * freqs
    cosine = jnp.cos(angle)[:, :, None, :]
    sine = jnp.sin(angle)[:, :, None, :]
    front = value_rows[..., :half]
    back = value_rows[..., half:]
    return jnp.concatenate([front * cosine - back * sine, back * cosine + front * sine], axis=-1)


def per_device(tokens, norm_gain, span_order, w_query, w_key, value_weight, w_out):
    sequence_batch, rows_dev, _ = tokens.shape
    head_size = HEAD_DIM
    query_heads = w_query.shape[1] // head_size
    key_heads = w_key.shape[1] // head_size
    group_width = query_heads // key_heads
    block_rows = rows_dev // 2
    total_rows = sequence_batch * rows_dev
    factor = 1.0 / math.sqrt(head_size)
    rank = lax.axis_index("ctx")
    whole = lax.all_gather(tokens, "tp", axis=2, tiled=True)
    normed = normalize(whole.reshape(total_rows, whole.shape[2]), norm_gain)
    query_pos = positions_of(span_order, rank * rows_dev, rows_dev, block_rows)
    latest = jnp.max(query_pos, axis=1)
    stat_shape = (sequence_batch, key_heads, group_width, rows_dev)
    initial = (
        jnp.full(stat_shape, masked_score, jnp.float32),
        jnp.zeros(stat_shape, jnp.float32),
        jnp.zeros(stat_shape + (head_size,), jnp.float32),
    )
    pieces = (
        lax.all_gather(w_query, "ctx", axis=0, tiled=True),
        lax.all_gather(w_key, "ctx", axis=0, tiled=True),
        lax.all_gather(value_weight, "ctx", axis=0, tiled=True),
    )
    query_flat, flattened_key, flattened_value = tuple(
        (jnp.dot(normed, piece, preferred_element_type=jnp.float32) for piece in pieces)
    )
    turned = apply_rotation(
        query_flat.reshape(sequence_batch, rows_dev, query_heads, head_size), query_pos, head_size
    ).astype(jnp.bfloat16)
    query = turned.reshape(sequence_batch, rows_dev, key_heads, group_width, head_size).transpose(
        0, 2, 3, 1, 4
    )
    turned = apply_rotation(
        flattened_key.reshape(sequence_batch, rows_dev, key_heads, head_size), query_pos, head_size
    ).astype(jnp.bfloat16)
    own_values = flattened_value.reshape(sequence_batch, rows_dev, key_heads, head_size).astype(
        jnp.bfloat16
    )
    key_piece = lax.all_gather(turned, "ctx", axis=1, tiled=True)
    value_piece = lax.all_gather(own_values, "ctx", axis=1, tiled=True)
    count = key_piece.shape[1]
    step_rows = 512

    def one_block(index, state):
        first = index * step_rows
        key_block = lax.dynamic_slice_in_dim(key_piece, first, step_rows, 1)
        value_block = lax.dynamic_slice_in_dim(value_piece, first, step_rows, 1)
        key_pos = positions_of(span_order, first, step_rows, block_rows)

        def update(current):
            peak, total, summed = current
            scores = (
                jnp.einsum(
                    "shgqd,skhd->shgqk", query, key_block, preferred_element_type=jnp.float32
                )
                * factor
            )
            allowed = key_pos[:, None, None, None, :] <= query_pos[:, None, None, :, None]
            scores = jnp.where(allowed, scores, masked_score)
            new_peak = jnp.maximum(peak, jnp.max(scores, axis=-1))
            weights = jnp.where(allowed, jnp.exp(scores - new_peak[..., None]), 0.0)
            shrink = jnp.exp(peak - new_peak)
            total = total * shrink + jnp.sum(weights, axis=-1)
            summed = summed * shrink[..., None] + jnp.einsum(
                "shgqk,skhd->shgqd",
                weights.astype(jnp.bfloat16),
                value_block,
                preferred_element_type=jnp.float32,
            )
            return (new_peak, total, summed)

        return lax.cond(
            jnp.all(jnp.min(key_pos, axis=1) > latest), lambda kept: kept, update, state
        )

    peak, total, summed = lax.fori_loop(0, count // step_rows, one_block, initial)
    attended = (summed / total[..., None]).astype(jnp.bfloat16)
    attended = attended.transpose(0, 3, 1, 2, 4).reshape(total_rows, query_heads * head_size)
    terms = jnp.dot(
        attended,
        lax.all_gather(w_out, "ctx", axis=1, tiled=True),
        preferred_element_type=jnp.float32,
    )
    mixed = lax.psum_scatter(terms.astype(jnp.bfloat16), "tp", scatter_dimension=1, tiled=True)
    return mixed.reshape(sequence_batch, rows_dev, mixed.shape[1])


def solution(mesh):
    placed = (
        P(None, "ctx", "tp"),
        P(),
        P(),
        P("ctx", "tp"),
        P("ctx", "tp"),
        P("ctx", "tp"),
        P("tp", "ctx"),
    )
    return jax.shard_map(
        per_device, mesh=mesh, in_specs=placed, out_specs=P(None, "ctx", "tp"), check_vma=False
    )
```

profile of v0, /device:TPU:0, one launch (start us, length us, event | category | flops | bytes accessed | tf_op | source)
XLA Modules:
  0.0 862.1 jit_solution(7252307660646929625)
XLA Ops:
  6.5 0.7 all-gather.10.cloned.1.call-update
  9.5 1.0 multiply_cosine_fusion
  10.5 48.0 %all-gather.10.cloned.1.call-done = bf16[8192,256]{1,0:T(8,128)(2,1)} async-done(((bf16[1024,256]{1,0:T(8,128)(2,1)}), bf16[8192,256]{1,0:T(8,128)(2,1)}) %all-gather.10.cloned.1.call-update) | async-done | bytes 4194320 | tf_op jit(solution)/shard_map/all_gather | solution.py:62
  58.6 6.3 copy.24
  64.9 151.7 %all-gather.8.cloned.1.call-done = bf16[2,512,8192]{2,1,0:T(8,128)(2,1)} async-done(((bf16[2,512,2048]{2,1,0:T(8,128)(2,1)}), bf16[2,512,8192]{2,1,0:T(8,128)(2,1)}) %all-gather.8.cloned.1.call-update) | async-done | bytes 16777232 | tf_op jit(solution)/shard_map/all_gather | solution.py:50
  216.5 7.5 fusion.21
  224.0 9.0 %fusion.29 = f32[2,512,2,128]{1,3,2,0:T(8,128)S(1)} fusion(bf16[2,128,8192,1]{2,1,0,3:T(8,128)(2,1)S(1)} %bitcast.69, bf16[2,512,8192]{2,1,0:T(8,128)(2,1)} %all-gather.8.cloned.1.call-done, f32[8192]{0:T(1024)S(1)} %copy-done.2, f32[2,512]{1,0:T(2,128)S(1)} %add_rsqrt_fusion), kind=kOutput, calls=%fused_computation.49 | convolution fusion | flops 4328521728 | bytes 22056960 | tf_op jit(solution)/shard_map/dot_general | solution.py:66
  233.3 0.9 pad_maximum_fusion
  234.2 30.9 %all-gather.16.cloned.1.call-done = bf16[8192,256]{1,0:T(8,128)(2,1)} async-done(((bf16[1024,256]{1,0:T(8,128)(2,1)}), bf16[8192,256]{1,0:T(8,128)(2,1)}) %all-gather.16.cloned.1.call-update) | async-done | bytes 4194320 | tf_op jit(solution)/shard_map/all_gather | solution.py:63
  265.1 6.3 copy.28
  271.4 12.7 %convolution_convert_fusion.1 = bf16[2,512,2,128]{3,1,2,0:T(8,128)(2,1)} fusion(bf16[2,128,8192,1]{2,1,0,3:T(8,128)(2,1)} %bitcast.70, bf16[2,512,8192]{2,1,0:T(8,128)(2,1)} %all-gather.8.cloned.1.call-done, f32[8192]{0:T(1024)S(1)} %copy-done.2, f32[2,512]{1,0:T(2,128)S(1)} %add_rsqrt_fusion), kind=kOutput, calls=%fused_computation.47 | convolution fusion | flops 4328783872 | bytes 21532672 | tf_op jit(solution)/shard_map/dot_general | solution.py:66
  285.2 131.2 %all-gather.14.cloned.1.call-done = bf16[8192,1024]{1,0:T(8,128)(2,1)} async-done(((bf16[1024,1024]{1,0:T(8,128)(2,1)}), bf16[8192,1024]{1,0:T(8,128)(2,1)}) %all-gather.14.cloned.1.call-update) | async-done | bytes 16777232 | tf_op jit(solution)/shard_map/all_gather | solution.py:61
  416.4 21.4 %copy.25 = bf16[1024,8192]{1,0:T(8,128)(2,1)} copy(bf16[1024,8192]{0,1:T(8,128)(2,1)} %bitcast.63) | data formatting | bytes 33554432 | tf_op jit(solution)/shard_map/dot_general | solution.py:66
  437.9 22.4 %fusion.27 = f32[2,512,8,128]{1,3,2,0:T(8,128)S(1)} fusion(bf16[8,128,8192,1]{2,1,0,3:T(8,128)(2,1)} %bitcast.64, bf16[2,512,8192]{2,1,0:T(8,128)(2,1)} %all-gather.8.cloned.1.call-done, f32[8192]{0:T(1024)S(1)} %copy-done.2, f32[2,512]{1,0:T(2,128)S(1)} %add_rsqrt_fusion), kind=kOutput, calls=%fused_computation.48 | convolution fusion | flops 17213423616 | bytes 37785600 | tf_op jit(solution)/shard_map/dot_general | solution.py:66
  460.2 1.7 subtract_convert_fusion
  462.0 2.0 copy.26
  464.0 1.8 copy.27
  465.8 4.1 maximum_bitcast_fusion
  469.9 6.4 copy.29
  476.3 33.8 %all-gather.18.cloned.1.call-done = bf16[2,4096,2,128]{3,1,2,0:T(8,128)(2,1)} async-done(((bf16[2,512,2,128]{3,1,2,0:T(8,128)(2,1)}), bf16[2,4096,2,128]{3,1,2,0:T(8,128)(2,1)}) %all-gather.18.cloned.1.call-update) | async-done | bytes 4194320 | tf_op jit(solution)/shard_map/all_gather | solution.py:81
  510.1 2.5 broadcast_in_dim.135
  512.6 156.1 %while.19 = (s32[]{:T(128)}, f32[2,2,4,512]{3,2,1,0:T(4,128)S(1)}, f32[2,2,4,512]{3,2,1,0:T(4,128)S(1)}, f32[2,2,4,512,128]{4,3,2,1,0:T(8,128)}, s32[2,16]{1,0:T...) while((s32[]{:T(128)}, f32[2,2,4,512]{3,2,1,0:T(4,128)S(1)}, ...), condition=%wide.region_11.12_spmd, body=%wide.region_3.11_spmd.sunk | while | flops 2204700672 | bytes 64532936 | solution.py:117
  512.9 0.7 compare_reduce_fusion.2
  514.2 17.9 %conditional.2 = (f32[2,2,4,512]{3,2,1,0:T(4,128)S(1)}, f32[2,2,4,512]{3,2,1,0:T(4,128)S(1)}, f32[2,2,4,512,128]{4,3,2,1,0:T(8,128)}) conditional(s32[]{:T(128)} %convert_element_type.85, (s32[2,512]{1,0:T(2,128)S(1)}, s32[2,512]{1,0:T(2,128)S(1)}, s32[]{:T(128)}, bf16[2,4096,2,128]{3,1,2,0:T(8,128)(2,1)}, bf16[2,2,4,512,128]{4,3,2,1,0:T(8,128)(2,1)}, ...), branch_computations={%region_7.9_spmd, %region_10.10_spmd} | conditional | flops 2204647424 | bytes 64430148 | solution.py:113
  514.6 4.7 fusion
  519.3 4.1 fusion.2
  523.5 8.7 %multiply_add_fusion = f32[2,2,4,512,128]{4,3,2,1,0:T(8,128)} fusion(f32[2,2,4,512,128]{4,3,2,1,0:T(8,128)} %get-tuple-element.360, f32[2,2,4,512]{3,2,1,0:T(4,128)S(1)} %bitcast.76, f32[2,2,512,4,512]{4,2,3,1,0:T(8,128)S(1)} %get-tuple-element.437, f32[2,2,4,512]{3,2,1,0:T(4,128)S(1)} %max.5, pred[2,512,512]{1,2,0:T(8,128)(4,1)S(1)} %broadcast_compare_fusion, ...), kind=kOutput, calls=%fused_computation.7 | convolution fusion | flops 1096810496 | bytes 26279940 | tf_op jit(solution)/shard_map/while/body/eval_jaxpr/cond/branch_0_fun/shgqk,skhd->shgqd/dot_general | solution.py:105
  532.4 0.7 compare_reduce_fusion.2
  533.8 17.9 %conditional.2 = (f32[2,2,4,512]{3,2,1,0:T(4,128)S(1)}, f32[2,2,4,512]{3,2,1,0:T(4,128)S(1)}, f32[2,2,4,512,128]{4,3,2,1,0:T(8,128)}) conditional(s32[]{:T(128)} %convert_element_type.85, (s32[2,512]{1,0:T(2,128)S(1)}, s32[2,512]{1,0:T(2,128)S(1)}, s32[]{:T(128)}, bf16[2,4096,2,128]{3,1,2,0:T(8,128)(2,1)}, bf16[2,2,4,512,128]{4,3,2,1,0:T(8,128)(2,1)}, ...), branch_computations={%region_7.9_spmd, %region_10.10_spmd} | conditional | flops 2204647424 | bytes 64430148 | solution.py:113
  534.2 4.7 fusion
  538.9 4.1 fusion.2
  543.0 8.7 %multiply_add_fusion = f32[2,2,4,512,128]{4,3,2,1,0:T(8,128)} fusion(f32[2,2,4,512,128]{4,3,2,1,0:T(8,128)} %get-tuple-element.360, f32[2,2,4,512]{3,2,1,0:T(4,128)S(1)} %bitcast.76, f32[2,2,512,4,512]{4,2,3,1,0:T(8,128)S(1)} %get-tuple-element.437, f32[2,2,4,512]{3,2,1,0:T(4,128)S(1)} %max.5, pred[2,512,512]{1,2,0:T(8,128)(4,1)S(1)} %broadcast_compare_fusion, ...), kind=kOutput, calls=%fused_computation.7 | convolution fusion | flops 1096810496 | bytes 26279940 | tf_op jit(solution)/shard_map/while/body/eval_jaxpr/cond/branch_0_fun/shgqk,skhd->shgqd/dot_general | solution.py:105
  553.3 17.9 %conditional.2 = (f32[2,2,4,512]{3,2,1,0:T(4,128)S(1)}, f32[2,2,4,512]{3,2,1,0:T(4,128)S(1)}, f32[2,2,4,512,128]{4,3,2,1,0:T(8,128)}) conditional(s32[]{:T(128)} %convert_element_type.85, (s32[2,512]{1,0:T(2,128)S(1)}, s32[2,512]{1,0:T(2,128)S(1)}, s32[]{:T(128)}, bf16[2,4096,2,128]{3,1,2,0:T(8,128)(2,1)}, bf16[2,2,4,512,128]{4,3,2,1,0:T(8,128)(2,1)}, ...), branch_computations={%region_7.9_spmd, %region_10.10_spmd} | conditional | flops 2204647424 | bytes 64430148 | solution.py:113
  553.7 4.7 fusion
  558.4 4.1 fusion.2
  562.5 8.7 %multiply_add_fusion = f32[2,2,4,512,128]{4,3,2,1,0:T(8,128)} fusion(f32[2,2,4,512,128]{4,3,2,1,0:T(8,128)} %get-tuple-element.360, f32[2,2,4,512]{3,2,1,0:T(4,128)S(1)} %bitcast.76, f32[2,2,512,4,512]{4,2,3,1,0:T(8,128)S(1)} %get-tuple-element.437, f32[2,2,4,512]{3,2,1,0:T(4,128)S(1)} %max.5, pred[2,512,512]{1,2,0:T(8,128)(4,1)S(1)} %broadcast_compare_fusion, ...), kind=kOutput, calls=%fused_computation.7 | convolution fusion | flops 1096810496 | bytes 26279940 | tf_op jit(solution)/shard_map/while/body/eval_jaxpr/cond/branch_0_fun/shgqk,skhd->shgqd/dot_general | solution.py:105
  571.4 0.7 compare_reduce_fusion.2
  572.8 17.9 %conditional.2 = (f32[2,2,4,512]{3,2,1,0:T(4,128)S(1)}, f32[2,2,4,512]{3,2,1,0:T(4,128)S(1)}, f32[2,2,4,512,128]{4,3,2,1,0:T(8,128)}) conditional(s32[]{:T(128)} %convert_element_type.85, (s32[2,512]{1,0:T(2,128)S(1)}, s32[2,512]{1,0:T(2,128)S(1)}, s32[]{:T(128)}, bf16[2,4096,2,128]{3,1,2,0:T(8,128)(2,1)}, bf16[2,2,4,512,128]{4,3,2,1,0:T(8,128)(2,1)}, ...), branch_computations={%region_7.9_spmd, %region_10.10_spmd} | conditional | flops 2204647424 | bytes 64430148 | solution.py:113
  573.2 4.7 fusion
  577.9 4.1 fusion.2
  582.0 8.7 %multiply_add_fusion = f32[2,2,4,512,128]{4,3,2,1,0:T(8,128)} fusion(f32[2,2,4,512,128]{4,3,2,1,0:T(8,128)} %get-tuple-element.360, f32[2,2,4,512]{3,2,1,0:T(4,128)S(1)} %bitcast.76, f32[2,2,512,4,512]{4,2,3,1,0:T(8,128)S(1)} %get-tuple-element.437, f32[2,2,4,512]{3,2,1,0:T(4,128)S(1)} %max.5, pred[2,512,512]{1,2,0:T(8,128)(4,1)S(1)} %broadcast_compare_fusion, ...), kind=kOutput, calls=%fused_computation.7 | convolution fusion | flops 1096810496 | bytes 26279940 | tf_op jit(solution)/shard_map/while/body/eval_jaxpr/cond/branch_0_fun/shgqk,skhd->shgqd/dot_general | solution.py:105
  592.3 17.9 %conditional.2 = (f32[2,2,4,512]{3,2,1,0:T(4,128)S(1)}, f32[2,2,4,512]{3,2,1,0:T(4,128)S(1)}, f32[2,2,4,512,128]{4,3,2,1,0:T(8,128)}) conditional(s32[]{:T(128)} %convert_element_type.85, (s32[2,512]{1,0:T(2,128)S(1)}, s32[2,512]{1,0:T(2,128)S(1)}, s32[]{:T(128)}, bf16[2,4096,2,128]{3,1,2,0:T(8,128)(2,1)}, bf16[2,2,4,512,128]{4,3,2,1,0:T(8,128)(2,1)}, ...), branch_computations={%region_7.9_spmd, %region_10.10_spmd} | conditional | flops 2204647424 | bytes 64430148 | solution.py:113
  592.7 4.8 fusion
  597.5 4.1 fusion.2
  601.7 8.6 multiply_add_fusion
  610.5 0.7 compare_reduce_fusion.2
  611.9 17.8 %conditional.2 = (f32[2,2,4,512]{3,2,1,0:T(4,128)S(1)}, f32[2,2,4,512]{3,2,1,0:T(4,128)S(1)}, f32[2,2,4,512,128]{4,3,2,1,0:T(8,128)}) conditional(s32[]{:T(128)} %convert_element_type.85, (s32[2,512]{1,0:T(2,128)S(1)}, s32[2,512]{1,0:T(2,128)S(1)}, s32[]{:T(128)}, bf16[2,4096,2,128]{3,1,2,0:T(8,128)(2,1)}, bf16[2,2,4,512,128]{4,3,2,1,0:T(8,128)(2,1)}, ...), branch_computations={%region_7.9_spmd, %region_10.10_spmd} | conditional | flops 2204647424 | bytes 64430148 | solution.py:113
  612.3 4.7 fusion
  617.0 4.1 fusion.2
  621.1 8.6 multiply_add_fusion
  631.4 17.8 %conditional.2 = (f32[2,2,4,512]{3,2,1,0:T(4,128)S(1)}, f32[2,2,4,512]{3,2,1,0:T(4,128)S(1)}, f32[2,2,4,512,128]{4,3,2,1,0:T(8,128)}) conditional(s32[]{:T(128)} %convert_element_type.85, (s32[2,512]{1,0:T(2,128)S(1)}, s32[2,512]{1,0:T(2,128)S(1)}, s32[]{:T(128)}, bf16[2,4096,2,128]{3,1,2,0:T(8,128)(2,1)}, bf16[2,2,4,512,128]{4,3,2,1,0:T(8,128)(2,1)}, ...), branch_computations={%region_7.9_spmd, %region_10.10_spmd} | conditional | flops 2204647424 | bytes 64430148 | solution.py:113
  631.7 4.7 fusion
  636.5 4.1 fusion.2
  640.6 8.6 multiply_add_fusion
  649.4 0.7 compare_reduce_fusion.2
  650.8 17.9 %conditional.2 = (f32[2,2,4,512]{3,2,1,0:T(4,128)S(1)}, f32[2,2,4,512]{3,2,1,0:T(4,128)S(1)}, f32[2,2,4,512,128]{4,3,2,1,0:T(8,128)}) conditional(s32[]{:T(128)} %convert_element_type.85, (s32[2,512]{1,0:T(2,128)S(1)}, s32[2,512]{1,0:T(2,128)S(1)}, s32[]{:T(128)}, bf16[2,4096,2,128]{3,1,2,0:T(8,128)(2,1)}, bf16[2,2,4,512,128]{4,3,2,1,0:T(8,128)(2,1)}, ...), branch_computations={%region_7.9_spmd, %region_10.10_spmd} | conditional | flops 2204647424 | bytes 64430148 | solution.py:113
  651.2 4.7 fusion
  655.9 4.1 fusion.2
  660.0 8.7 %multiply_add_fusion = f32[2,2,4,512,128]{4,3,2,1,0:T(8,128)} fusion(f32[2,2,4,512,128]{4,3,2,1,0:T(8,128)} %get-tuple-element.360, f32[2,2,4,512]{3,2,1,0:T(4,128)S(1)} %bitcast.76, f32[2,2,512,4,512]{4,2,3,1,0:T(8,128)S(1)} %get-tuple-element.437, f32[2,2,4,512]{3,2,1,0:T(4,128)S(1)} %max.5, pred[2,512,512]{1,2,0:T(8,128)(4,1)S(1)} %broadcast_compare_fusion, ...), kind=kOutput, calls=%fused_computation.7 | convolution fusion | flops 1096810496 | bytes 26279940 | tf_op jit(solution)/shard_map/while/body/eval_jaxpr/cond/branch_0_fun/shgqk,skhd->shgqd/dot_general | solution.py:105
  668.7 3.1 fusion.25
  671.8 1.6 copy.30
  673.4 2.7 reshape.213
  676.1 26.4 %convolution_convert_fusion = bf16[1024,8192]{1,0:T(8,128)(2,1)} fusion(bf16[1024,1024]{1,0:T(8,128)(2,1)} %reshape.213, bf16[1024,8192]{1,0:T(8,128)(2,1)} %all-gather.20.cloned.1.call-done), kind=kOutput, calls=%fused_computation.41 | convolution fusion | flops 17188257792 | bytes 35651584 | tf_op jit(solution)/shard_map/dot_general | solution.py:120
  702.6 152.7 %reduce-scatter.2.cloned.1.call-done = bf16[1024,2048]{1,0:T(8,128)(2,1)} async-done(((bf16[1024,8192]{1,0:T(8,128)(2,1)}), bf16[1024,2048]{1,0:T(8,128)(2,1)}) %reduce-scatter.2.cloned.1.call-update) | async-done | bytes 4194320 | tf_op jit(solution)/shard_map/reduce_scatter | solution.py:125
  (100 shorter events, 10.8 us)
Async XLA Ops:
  6.5 2.9 copy-start.1
  6.5 52.0 %all-gather.10.cloned.1.call-start = ((), (), s32[]{:S(2)}) async-start(), calls=%async_computation.2 | async-start | bytes 4718592 | tf_op jit(solution)/shard_map/all_gather | solution.py:62
  7.3 209.3 %all-gather.8.cloned.1.call-start = ((), (), s32[]{:S(2)}) async-start(), calls=%async_computation.1 | async-start | bytes 20971520 | tf_op jit(solution)/shard_map/all_gather | solution.py:50
  8.0 257.0 %all-gather.16.cloned.1.call-start = ((), (), s32[]{:S(2)}) async-start(), calls=%async_computation.5 | async-start | bytes 4718592 | tf_op jit(solution)/shard_map/all_gather | solution.py:63
  8.7 407.7 %all-gather.14.cloned.1.call-start = ((), (), s32[]{:S(2)}) async-start(), calls=%async_computation.4 | async-start | bytes 18874368 | tf_op jit(solution)/shard_map/all_gather | solution.py:61
  9.3 460.5 %all-gather.12.cloned.1.call-start = ((), (), s32[]{:S(2)}) async-start(), calls=%async_computation.3 | async-start | bytes 4718592 | tf_op jit(solution)/shard_map/all_gather | solution.py:80
  64.9 159.1 %copy-start.2 = (f32[8192]{0:T(1024)S(1)}, f32[8192]{0:T(1024)}, u32[]{:S(2)}) copy-start(f32[8192]{0:T(1024)} %param.12) | copy-start | bytes 98308
  216.5 7.5 copy-start
  234.1 276.0 %all-gather.18.cloned.1.call-start = ((), (), s32[]{:S(2)}) async-start(), calls=%async_computation.6 | async-start | bytes 4718592 | tf_op jit(solution)/shard_map/all_gather | solution.py:81
  284.1 392.1 %all-gather.20.cloned.1.call-start = ((), (), s32[]{:S(2)}) async-start(), calls=%async_computation.7 | async-start | bytes 18874368 | tf_op jit(solution)/shard_map/all_gather | solution.py:122
  284.8 570.4 %reduce-scatter.2.cloned.1.call-start = ((), (), s32[]{:S(2)}) async-start(), calls=%async_computation.8 | async-start | bytes 20971520 | tf_op jit(solution)/shard_map/reduce_scatter | solution.py:125
Sparse Core Ops, SparseCore 0:
  8.9 49.5 all-gather.9
  60.4 156.0 all-gather.7
  218.1 46.8 all-gather.15
  266.5 149.8 all-gather.13
  417.9 45.0 all-gather.11
  464.4 45.6 all-gather.17
  511.7 149.8 all-gather.19
  702.7 152.5 reduce-scatter.1
where the time goes:
time: 864 us; the launch traced here: 862 us
  waiting for transfers between devices  552 us (64%)
  matrix products  177 us (20%)
  other arithmetic  62 us (7%)
  local copies, waits for them, and re-layouts  51.1 us (6%)
  between operations  13.6 us (2%)
    reduce_scatter x1, waiting for transfers between devices, per_device(): lax.psum_scatter(terms.astype(jnp.bfloat16), 'tp', scatter_dimension=1, t...  153 us
    all_gather x1, waiting for transfers between devices, per_device(): whole = lax.all_gather(tokens, 'tp', axis=2, tiled=True)  152 us
    all_gather x1, waiting for transfers between devices, per_device(): lax.all_gather(w_query, 'ctx', axis=0, tiled=True)  131 us
    dot_general x8, matrix products, update(): jnp.einsum('shgqk,skhd->shgqd', weights.astype(jnp.bfloat16), value_block...  69.1 us
    all_gather x1, waiting for transfers between devices, per_device(): lax.all_gather(w_key, 'ctx', axis=0, tiled=True)  48 us
    dot_general x3, matrix products, per_device(): jnp.dot(normed, piece, preferred_element_type=jnp.float32)  44.1 us
    dot_general x8, matrix products, update(): jnp.einsum('shgqd,skhd->shgqk', query, key_block, preferred_element_type=...  37.6 us
    dot_general x3, local copies, waits for them, and re-layouts, per_device(): jnp.dot(normed, piece, preferred_element_type=jnp.float32)  34.1 us
  transfers between devices with their start and end apart: 8, of which 6 were waited for; matrix products, arithmetic and copies ran while one was open for 31% of the time, Pallas kernels for 0%

commit v1 on v0

--- a/solution.py
+++ b/solution.py
@@ -8,6 +8,19 @@
 theta_base = 500000.0
 norm_eps = 1e-05
 masked_score = -1e30
+
+
+def ring_gather(x, axis, dim):
+    ways = lax.axis_size(axis)
+    up = [(d, (d + 1) % ways) for d in range(ways)]
+    down = [(d, (d - 1) % ways) for d in range(ways)]
+    earlier, later = ([x], [x])
+    for _ in range(ways // 2):
+        earlier.append(lax.ppermute(earlier[-1], axis, up))
+    for _ in range((ways - 1) // 2):
+        later.append(lax.ppermute(later[-1], axis, down))
+    line = jnp.concatenate([*earlier[::-1], *later[1:]], axis=dim)
+    return jnp.roll(line, (lax.axis_index(axis) - ways // 2) * x.shape[dim], axis=dim)
 
 
 def normalize(flat_rows, norm_gain):
@@ -58,7 +71,7 @@
         jnp.zeros(stat_shape + (head_size,), jnp.float32),
     )
     pieces = (
-        lax.all_gather(w_query, "ctx", axis=0, tiled=True),
+        ring_gather(w_query, "ctx", 0),
         lax.all_gather(w_key, "ctx", axis=0, tiled=True),
         lax.all_gather(value_weight, "ctx", axis=0, tiled=True),
     )

time: 864 us -> 1080 us (1.25)
  waiting for transfers between devices: 552 us -> 734 us
  local copies, waits for them, and re-layouts: 51.1 us -> 77.1 us
    ppermute x0 -> x7, waiting for transfers between devices: none -> 296 us  [the longest x4 289 us: ring_gather(): earlier.append(lax.ppermute(earlier[-1], axis, up))]
    all_gather x1 -> x0, waiting for transfers between devices: 131 us -> none  [per_device(): lax.all_gather(w_query, 'ctx', axis=0, tiled=True)]
    reduce_scatter x1, waiting for transfers between devices: 153 us -> 205 us  [per_device(): lax.psum_scatter(terms.astype(jnp.bfloat16), 'tp', scatter_dimension=1, t...]
    all_gather x1, waiting for transfers between devices: 33.8 us -> 0.01 us  [per_device(): value_piece = lax.all_gather(own_values, 'ctx', axis=1, tiled=True)]
    unnamed x6 -> x39, local copies, waits for them, and re-layouts: 0.01 us -> 17.4 us
    ppermute x0 -> x7, starting transfers between devices: none -> 11 us  [the longest x3 10.7 us: ring_gather(): later.append(lax.ppermute(later[-1], axis, down))]
    dot_general x3 -> x4, local copies, waits for them, and re-layouts: 34.1 us -> 41.1 us  [per_device(): jnp.dot(normed, piece, preferred_element_type=jnp.float32)]
  transfers between devices with their start and end apart: 8 -> 14, of which waited for: 6 -> 9; matrix products, arithmetic and copies ran while one was open for 31% -> 27% of each run, Pallas kernels for 0% -> 0%
where the time goes in v1:
time: 1080 us
  waiting for transfers between devices  734 us (68%)
  matrix products  175 us (16%)
  local copies, waits for them, and re-layouts  77.1 us (7%)
  other arithmetic  62.5 us (6%)
  between operations  13.8 us (1%)
  starting transfers between devices  11.2 us (1%)
    ppermute x4, waiting for transfers between devices, ring_gather(): earlier.append(lax.ppermute(earlier[-1], axis, up))  289 us
    reduce_scatter x1, waiting for transfers between devices, per_device(): lax.psum_scatter(terms.astype(jnp.bfloat16), 'tp', scatter_dimension=1, t...  205 us
    all_gather x1, waiting for transfers between devices, per_device(): whole = lax.all_gather(tokens, 'tp', axis=2, tiled=True)  152 us
    dot_general x8, matrix products, update(): jnp.einsum('shgqk,skhd->shgqd', weights.astype(jnp.bfloat16), value_block...  68.8 us
    all_gather x1, waiting for transfers between devices, per_device(): lax.all_gather(w_key, 'ctx', axis=0, tiled=True)  47.9 us
    dot_general x3, matrix products, per_device(): jnp.dot(normed, piece, preferred_element_type=jnp.float32)  42.2 us
    dot_general x4, local copies, waits for them, and re-layouts, per_device(): jnp.dot(normed, piece, preferred_element_type=jnp.float32)  41.1 us
    dot_general x8, matrix products, update(): jnp.einsum('shgqd,skhd->shgqk', query, key_block, preferred_element_type=...  37.5 us
  transfers between devices with their start and end apart: 14, of which 9 were waited for; matrix products, arithmetic and copies ran while one was open for 27% of the time, Pallas kernels for 0%

profile of v1, /device:TPU:0, one launch (start us, length us, event | category | flops | bytes accessed | tf_op | source)
XLA Modules:
  0.0 1079.2 jit_solution(13919498866640632862)
XLA Ops:
  10.6 47.9 %all-gather.9.cloned.1.call-done = bf16[8192,256]{1,0:T(8,128)(2,1)} async-done(((bf16[1024,256]{1,0:T(8,128)(2,1)}), bf16[8192,256]{1,0:T(8,128)(2,1)}) %all-gather.9.cloned.1.call-update) | async-done | bytes 4194320 | tf_op jit(solution)/shard_map/all_gather | solution.py:75
  58.6 6.3 copy.24
  64.9 151.7 %all-gather.7.cloned.1.call-done = bf16[2,512,8192]{2,1,0:T(8,128)(2,1)} async-done(((bf16[2,512,2048]{2,1,0:T(8,128)(2,1)}), bf16[2,512,8192]{2,1,0:T(8,128)(2,1)}) %all-gather.7.cloned.1.call-update) | async-done | bytes 16777232 | tf_op jit(solution)/shard_map/all_gather | solution.py:63
  216.5 7.5 fusion.21
  224.0 9.0 fusion.29
  234.2 30.8 %all-gather.13.cloned.1.call-done = bf16[8192,256]{1,0:T(8,128)(2,1)} async-done(((bf16[1024,256]{1,0:T(8,128)(2,1)}), bf16[8192,256]{1,0:T(8,128)(2,1)}) %all-gather.13.cloned.1.call-update) | async-done | bytes 4194320 | tf_op jit(solution)/shard_map/all_gather | solution.py:76
  265.1 6.3 copy.28
  271.4 10.9 %convolution_convert_fusion.1 = bf16[2,512,2,128]{3,1,2,0:T(8,128)(2,1)} fusion(bf16[2,128,8192,1]{2,1,0,3:T(8,128)(2,1)} %bitcast.70, bf16[2,512,8192]{2,1,0:T(8,128)(2,1)} %all-gather.7.cloned.1.call-done, f32[8192]{0:T(1024)S(1)} %copy-done.11, f32[2,512]{1,0:T(2,128)S(1)} %add_rsqrt_fusion), kind=kOutput, calls=%fused_computation.48 | convolution fusion | flops 4328783872 | bytes 21532672 | tf_op jit(solution)/shard_map/dot_general | solution.py:79
  283.2 50.6 %collective-permute-done = bf16[1024,1024]{1,0:T(8,128)(2,1)S(1)} collective-permute-done((bf16[1024,1024]{1,0:T(8,128)(2,1)S(1)}, bf16[1024,1024]{1,0:T(8,128)(2,1)S(1)}, u32[]{:S(2)}, u32[]{:S(2)}) %collective-permute-start) | collective-permute-done | bytes 2097184 | tf_op jit(solution)/shard_map/ppermute | solution.py:19
  333.8 3.5 collective-permute-start.4
  337.3 77.9 %collective-permute-done.1 = bf16[1024,1024]{1,0:T(8,128)(2,1)S(1)} collective-permute-done((bf16[1024,1024]{1,0:T(8,128)(2,1)S(1)}, bf16[1024,1024]{1,0:T(8,128)(2,1)S(1)}, u32[]{:S(2)}, u32[]{:S(2)}) %collective-permute-start.1) | collective-permute-done | bytes 2097184 | tf_op jit(solution)/shard_map/ppermute | solution.py:19
  415.3 3.6 collective-permute-start.5
  418.9 90.8 %collective-permute-done.2 = bf16[1024,1024]{1,0:T(8,128)(2,1)} collective-permute-done((bf16[1024,1024]{1,0:T(8,128)(2,1)S(1)}, bf16[1024,1024]{1,0:T(8,128)(2,1)}, u32[]{:S(2)}, u32[]{:S(2)}) %collective-permute-start.2) | collective-permute-done | bytes 2097184 | tf_op jit(solution)/shard_map/ppermute | solution.py:19
  509.7 3.5 collective-permute-start.6
  513.4 70.0 %collective-permute-done.3 = bf16[1024,1024]{1,0:T(8,128)(2,1)} collective-permute-done((bf16[1024,1024]{1,0:T(8,128)(2,1)}, bf16[1024,1024]{1,0:T(8,128)(2,1)}, u32[]{:S(2)}, u32[]{:S(2)}) %collective-permute-start.3) | collective-permute-done | bytes 2097184 | tf_op jit(solution)/shard_map/ppermute | solution.py:19
  585.1 1.8 constant_dynamic-update-slice_fusion.14
  586.9 2.0 constant_dynamic-update-slice_fusion.13
  588.9 1.9 constant_dynamic-update-slice_fusion.12
  592.9 6.9 collective-permute-done.6
  601.6 1.8 constant_dynamic-update-slice_fusion.7
  609.5 7.0 dynamic-slice_bitcast_fusion
  616.5 21.5 %copy.25 = bf16[1024,8192]{1,0:T(8,128)(2,1)} copy(bf16[1024,8192]{0,1:T(8,128)(2,1)} %dynamic-slice_bitcast_fusion) | data formatting | bytes 33554432 | tf_op jit(solution)/shard_map/dot_general | solution.py:79
  637.9 22.3 %fusion.27 = f32[2,512,8,128]{1,3,2,0:T(8,128)S(1)} fusion(bf16[8,128,8192,1]{2,1,0,3:T(8,128)(2,1)} %bitcast.64, bf16[2,512,8192]{2,1,0:T(8,128)(2,1)} %all-gather.7.cloned.1.call-done, f32[8192]{0:T(1024)S(1)} %copy-done.11, f32[2,512]{1,0:T(2,128)S(1)} %add_rsqrt_fusion), kind=kOutput, calls=%fused_computation.49 | convolution fusion | flops 17213423616 | bytes 37785600 | tf_op jit(solution)/shard_map/dot_general | solution.py:79
  662.0 2.0 copy.26
  665.8 4.1 maximum_bitcast_fusion
  669.9 6.3 copy.29
  676.3 2.5 broadcast_in_dim.135
  678.8 155.0 %while.19 = (s32[]{:T(128)}, f32[2,2,4,512]{3,2,1,0:T(4,128)S(1)}, f32[2,2,4,512]{3,2,1,0:T(4,128)S(1)}, f32[2,2,4,512,128]{4,3,2,1,0:T(8,128)}, s32[2,16]{1,0:T...) while((s32[]{:T(128)}, f32[2,2,4,512]{3,2,1,0:T(4,128)S(1)}, ...), condition=%wide.region_11.12_spmd, body=%wide.region_3.11_spmd.sunk | while | flops 2204700672 | bytes 64532936 | solution.py:130
  680.3 17.8 %conditional.2 = (f32[2,2,4,512]{3,2,1,0:T(4,128)S(1)}, f32[2,2,4,512]{3,2,1,0:T(4,128)S(1)}, f32[2,2,4,512,128]{4,3,2,1,0:T(8,128)}) conditional(s32[]{:T(128)} %convert_element_type.85, (s32[2,512]{1,0:T(2,128)S(1)}, s32[2,512]{1,0:T(2,128)S(1)}, s32[]{:T(128)}, bf16[2,4096,2,128]{3,1,2,0:T(8,128)(2,1)}, bf16[2,2,4,512,128]{4,3,2,1,0:T(8,128)(2,1)}, ...), branch_computations={%region_7.9_spmd, %region_10.10_spmd} | conditional | flops 2204647424 | bytes 64430148 | solution.py:126
  680.7 4.7 fusion
  685.4 4.1 fusion.2
  689.6 8.6 multiply_add_fusion
  699.7 17.8 %conditional.2 = (f32[2,2,4,512]{3,2,1,0:T(4,128)S(1)}, f32[2,2,4,512]{3,2,1,0:T(4,128)S(1)}, f32[2,2,4,512,128]{4,3,2,1,0:T(8,128)}) conditional(s32[]{:T(128)} %convert_element_type.85, (s32[2,512]{1,0:T(2,128)S(1)}, s32[2,512]{1,0:T(2,128)S(1)}, s32[]{:T(128)}, bf16[2,4096,2,128]{3,1,2,0:T(8,128)(2,1)}, bf16[2,2,4,512,128]{4,3,2,1,0:T(8,128)(2,1)}, ...), branch_computations={%region_7.9_spmd, %region_10.10_spmd} | conditional | flops 2204647424 | bytes 64430148 | solution.py:126
  700.1 4.7 fusion
  704.8 4.1 fusion.2
  708.9 8.6 multiply_add_fusion
  719.1 17.8 %conditional.2 = (f32[2,2,4,512]{3,2,1,0:T(4,128)S(1)}, f32[2,2,4,512]{3,2,1,0:T(4,128)S(1)}, f32[2,2,4,512,128]{4,3,2,1,0:T(8,128)}) conditional(s32[]{:T(128)} %convert_element_type.85, (s32[2,512]{1,0:T(2,128)S(1)}, s32[2,512]{1,0:T(2,128)S(1)}, s32[]{:T(128)}, bf16[2,4096,2,128]{3,1,2,0:T(8,128)(2,1)}, bf16[2,2,4,512,128]{4,3,2,1,0:T(8,128)(2,1)}, ...), branch_computations={%region_7.9_spmd, %region_10.10_spmd} | conditional | flops 2204647424 | bytes 64430148 | solution.py:126
  719.5 4.7 fusion
  724.2 4.1 fusion.2
  728.3 8.6 multiply_add_fusion
  738.5 17.8 %conditional.2 = (f32[2,2,4,512]{3,2,1,0:T(4,128)S(1)}, f32[2,2,4,512]{3,2,1,0:T(4,128)S(1)}, f32[2,2,4,512,128]{4,3,2,1,0:T(8,128)}) conditional(s32[]{:T(128)} %convert_element_type.85, (s32[2,512]{1,0:T(2,128)S(1)}, s32[2,512]{1,0:T(2,128)S(1)}, s32[]{:T(128)}, bf16[2,4096,2,128]{3,1,2,0:T(8,128)(2,1)}, bf16[2,2,4,512,128]{4,3,2,1,0:T(8,128)(2,1)}, ...), branch_computations={%region_7.9_spmd, %region_10.10_spmd} | conditional | flops 2204647424 | bytes 64430148 | solution.py:126
  738.8 4.7 fusion
  743.6 4.1 fusion.2
  747.7 8.6 multiply_add_fusion
  757.8 17.8 %conditional.2 = (f32[2,2,4,512]{3,2,1,0:T(4,128)S(1)}, f32[2,2,4,512]{3,2,1,0:T(4,128)S(1)}, f32[2,2,4,512,128]{4,3,2,1,0:T(8,128)}) conditional(s32[]{:T(128)} %convert_element_type.85, (s32[2,512]{1,0:T(2,128)S(1)}, s32[2,512]{1,0:T(2,128)S(1)}, s32[]{:T(128)}, bf16[2,4096,2,128]{3,1,2,0:T(8,128)(2,1)}, bf16[2,2,4,512,128]{4,3,2,1,0:T(8,128)(2,1)}, ...), branch_computations={%region_7.9_spmd, %region_10.10_spmd} | conditional | flops 2204647424 | bytes 64430148 | solution.py:126
  758.2 4.7 fusion
  762.9 4.1 fusion.2
  767.1 8.6 multiply_add_fusion
  777.2 17.8 %conditional.2 = (f32[2,2,4,512]{3,2,1,0:T(4,128)S(1)}, f32[2,2,4,512]{3,2,1,0:T(4,128)S(1)}, f32[2,2,4,512,128]{4,3,2,1,0:T(8,128)}) conditional(s32[]{:T(128)} %convert_element_type.85, (s32[2,512]{1,0:T(2,128)S(1)}, s32[2,512]{1,0:T(2,128)S(1)}, s32[]{:T(128)}, bf16[2,4096,2,128]{3,1,2,0:T(8,128)(2,1)}, bf16[2,2,4,512,128]{4,3,2,1,0:T(8,128)(2,1)}, ...), branch_computations={%region_7.9_spmd, %region_10.10_spmd} | conditional | flops 2204647424 | bytes 64430148 | solution.py:126
  777.6 4.7 fusion
  782.3 4.1 fusion.2
  786.4 8.6 multiply_add_fusion
  796.6 17.8 %conditional.2 = (f32[2,2,4,512]{3,2,1,0:T(4,128)S(1)}, f32[2,2,4,512]{3,2,1,0:T(4,128)S(1)}, f32[2,2,4,512,128]{4,3,2,1,0:T(8,128)}) conditional(s32[]{:T(128)} %convert_element_type.85, (s32[2,512]{1,0:T(2,128)S(1)}, s32[2,512]{1,0:T(2,128)S(1)}, s32[]{:T(128)}, bf16[2,4096,2,128]{3,1,2,0:T(8,128)(2,1)}, bf16[2,2,4,512,128]{4,3,2,1,0:T(8,128)(2,1)}, ...), branch_computations={%region_7.9_spmd, %region_10.10_spmd} | conditional | flops 2204647424 | bytes 64430148 | solution.py:126
  797.0 4.7 fusion
  801.7 4.1 fusion.2
  805.8 8.6 multiply_add_fusion
  816.0 17.8 %conditional.2 = (f32[2,2,4,512]{3,2,1,0:T(4,128)S(1)}, f32[2,2,4,512]{3,2,1,0:T(4,128)S(1)}, f32[2,2,4,512,128]{4,3,2,1,0:T(8,128)}) conditional(s32[]{:T(128)} %convert_element_type.85, (s32[2,512]{1,0:T(2,128)S(1)}, s32[2,512]{1,0:T(2,128)S(1)}, s32[]{:T(128)}, bf16[2,4096,2,128]{3,1,2,0:T(8,128)(2,1)}, bf16[2,2,4,512,128]{4,3,2,1,0:T(8,128)(2,1)}, ...), branch_computations={%region_7.9_spmd, %region_10.10_spmd} | conditional | flops 2204647424 | bytes 64430148 | solution.py:126
  816.3 4.7 fusion
  821.1 4.1 fusion.2
  825.2 8.6 multiply_add_fusion
  833.8 3.1 fusion.25
  838.5 2.7 reshape.213
  841.2 26.4 %convolution_convert_fusion = bf16[1024,8192]{1,0:T(8,128)(2,1)} fusion(bf16[1024,1024]{1,0:T(8,128)(2,1)} %reshape.213, bf16[1024,8192]{1,0:T(8,128)(2,1)} %all-gather.17.cloned.1.call-done), kind=kOutput, calls=%fused_computation.42 | convolution fusion | flops 17188257792 | bytes 35651584 | tf_op jit(solution)/shard_map/dot_general | solution.py:133
  867.6 204.7 %reduce-scatter.2.cloned.1.call-done = bf16[1024,2048]{1,0:T(8,128)(2,1)} async-done(((bf16[1024,8192]{1,0:T(8,128)(2,1)}), bf16[1024,2048]{1,0:T(8,128)(2,1)}) %reduce-scatter.2.cloned.1.call-update) | async-done | bytes 4194320 | tf_op jit(solution)/shard_map/reduce_scatter | solution.py:138
  (146 shorter events, 33.5 us)
Async XLA Ops:
  6.5 217.5 %copy-start.11 = (f32[8192]{0:T(1024)S(1)}, f32[8192]{0:T(1024)}, u32[]{:S(2)}) copy-start(f32[8192]{0:T(1024)} %param.12) | copy-start | bytes 98308
  6.5 52.0 %all-gather.9.cloned.1.call-start = ((), (), s32[]{:S(2)}) async-start(), calls=%async_computation.2 | async-start | bytes 4718592 | tf_op jit(solution)/shard_map/all_gather | solution.py:75
  7.3 209.3 %all-gather.7.cloned.1.call-start = ((), (), s32[]{:S(2)}) async-start(), calls=%async_computation.1 | async-start | bytes 20971520 | tf_op jit(solution)/shard_map/all_gather | solution.py:63
  8.0 257.0 %all-gather.13.cloned.1.call-start = ((), (), s32[]{:S(2)}) async-start(), calls=%async_computation.4 | async-start | bytes 4718592 | tf_op jit(solution)/shard_map/all_gather | solution.py:76
  8.7 661.2 %all-gather.11.cloned.1.call-start = ((), (), s32[]{:S(2)}) async-start(), calls=%async_computation.3 | async-start | bytes 4718592 | tf_op jit(solution)/shard_map/all_gather | solution.py:93
  10.6 222.4 %copy-start.8 = (f32[2,512,64]{1,2,0:T(8,128)}, f32[2,512,64]{1,2,0:T(8,128)S(1)}, u32[]{:S(2)}) copy-start(f32[2,512,64]{1,2,0:T(8,128)S(1)} %get-tuple-element.445) | copy-start | bytes 786436
  216.5 7.5 copy-start.7
  234.2 442.1 %all-gather.15.cloned.1.call-start = ((), (), s32[]{:S(2)}) async-start(), calls=%async_computation.5 | async-start | bytes 4718592 | tf_op jit(solution)/shard_map/all_gather | solution.py:94
  271.4 11.5 %copy-start = (bf16[1024,1024]{1,0:T(8,128)(2,1)S(1)}, bf16[1024,1024]{1,0:T(8,128)(2,1)}, u32[]{:S(2)}) copy-start(bf16[1024,1024]{1,0:T(8,128)(2,1)} %param.14) | copy-start | bytes 6291460
  282.3 558.9 %all-gather.17.cloned.1.call-start = ((), (), s32[]{:S(2)}) async-start(), calls=%async_computation.6 | async-start | bytes 18874368 | tf_op jit(solution)/shard_map/all_gather | solution.py:135
  282.8 789.5 %reduce-scatter.2.cloned.1.call-start = ((), (), s32[]{:S(2)}) async-start(), calls=%async_computation.7 | async-start | bytes 20971520 | tf_op jit(solution)/shard_map/reduce_scatter | solution.py:138
  282.9 50.9 %collective-permute-start = (bf16[1024,1024]{1,0:T(8,128)(2,1)S(1)}, bf16[1024,1024]{1,0:T(8,128)(2,1)S(1)}, u32[]{:S(2)}, u32[]{:S(2)}) collective-permute-start(bf16[1024,1024]{1,0:T(8,128)(2,1)S(1)} %copy-done), channel_id=1, source_target_pairs={{0,4},{4,8},{8,12},{12,16},{16,20},{20,24},{24,28},{28,0},{1,5},{5... | collective-permute-start | bytes 6291464 | tf_op jit(solution)/shard_map/ppermute | solution.py:19
  333.8 81.5 %copy-start.1 = (bf16[1024,1024]{1,0:T(8,128)(2,1)}, bf16[1024,1024]{1,0:T(8,128)(2,1)S(1)}, u32[]{:S(2)}) copy-start(bf16[1024,1024]{1,0:T(8,128)(2,1)S(1)} %collective-permute-done) | copy-start | bytes 6291460
  333.8 81.5 %collective-permute-start.1 = (bf16[1024,1024]{1,0:T(8,128)(2,1)S(1)}, bf16[1024,1024]{1,0:T(8,128)(2,1)S(1)}, u32[]{:S(2)}, u32[]{:S(2)}) collective-permute-start(bf16[1024,1024]{1,0:T(8,128)(2,1)S(1)} %collective-permute-done), channel_id=1, source_target_pairs={{0,4},{4,8},{8,12},{12,16},{16,20},{20,24},{24,28},{28,0},{1,5},{5... | collective-permute-start | bytes 6291464 | tf_op jit(solution)/shard_map/ppermute | solution.py:19
  333.8 81.5 %collective-permute-start.4 = (bf16[1024,1024]{1,0:T(8,128)(2,1)S(1)}, bf16[1024,1024]{1,0:T(8,128)(2,1)S(1)}, u32[]{:S(2)}, u32[]{:S(2)}) collective-permute-start(bf16[1024,1024]{1,0:T(8,128)(2,1)S(1)} %copy-done), channel_id=1, source_target_pairs={{0,28},{4,0},{8,4},{12,8},{16,12},{20,16},{24,20},{28,24},{1,29},{... | collective-permute-start | bytes 6291464 | tf_op jit(solution)/shard_map/ppermute | solution.py:21
  415.3 94.4 %copy-start.5 = (bf16[1024,1024]{1,0:T(8,128)(2,1)}, bf16[1024,1024]{1,0:T(8,128)(2,1)S(1)}, u32[]{:S(2)}) copy-start(bf16[1024,1024]{1,0:T(8,128)(2,1)S(1)} %collective-permute-done.1) | copy-start | bytes 6291460
  415.3 94.4 %collective-permute-start.2 = (bf16[1024,1024]{1,0:T(8,128)(2,1)S(1)}, bf16[1024,1024]{1,0:T(8,128)(2,1)}, u32[]{:S(2)}, u32[]{:S(2)}) collective-permute-start(bf16[1024,1024]{1,0:T(8,128)(2,1)S(1)} %collective-permute-done.1), channel_id=1, source_target_pairs={{0,4},{4,8},{8,12},{12,16},{16,20},{20,24},{24,28},{28,0},{1,5},{5... | collective-permute-start | bytes 6291464 | tf_op jit(solution)/shard_map/ppermute | solution.py:19
  415.3 3.6 copy-start.3
  415.3 94.4 %collective-permute-start.5 = (bf16[1024,1024]{1,0:T(8,128)(2,1)S(1)}, bf16[1024,1024]{1,0:T(8,128)(2,1)}, u32[]{:S(2)}, u32[]{:S(2)}) collective-permute-start(bf16[1024,1024]{1,0:T(8,128)(2,1)S(1)} %collective-permute-done.4), channel_id=1, source_target_pairs={{0,28},{4,0},{8,4},{12,8},{16,12},{20,16},{24,20},{28,24},{1,29},{... | collective-permute-start | bytes 6291464 | tf_op jit(solution)/shard_map/ppermute | solution.py:21
  509.7 73.6 %collective-permute-start.3 = (bf16[1024,1024]{1,0:T(8,128)(2,1)}, bf16[1024,1024]{1,0:T(8,128)(2,1)}, u32[]{:S(2)}, u32[]{:S(2)}) collective-permute-start(bf16[1024,1024]{1,0:T(8,128)(2,1)} %collective-permute-done.2), channel_id=1, source_target_pairs={{0,4},{4,8},{8,12},{12,16},{16,20},{20,24},{24,28},{28,0},{1,5},{5... | collective-permute-start | bytes 6291464 | tf_op jit(solution)/shard_map/ppermute | solution.py:19
  509.7 90.1 %collective-permute-start.6 = (bf16[1024,1024]{1,0:T(8,128)(2,1)}, bf16[1024,1024]{1,0:T(8,128)(2,1)}, u32[]{:S(2)}, u32[]{:S(2)}) collective-permute-start(bf16[1024,1024]{1,0:T(8,128)(2,1)} %collective-permute-done.5), channel_id=1, source_target_pairs={{0,28},{4,0},{8,4},{12,8},{16,12},{20,16},{24,20},{28,24},{1,29},{... | collective-permute-start | bytes 6291464 | tf_op jit(solution)/shard_map/ppermute | solution.py:21
  513.4 77.6 %copy-start.4 = (bf16[1024,1024]{1,0:T(8,128)(2,1)S(1)}, bf16[1024,1024]{1,0:T(8,128)(2,1)}, u32[]{:S(2)}) copy-start(bf16[1024,1024]{1,0:T(8,128)(2,1)} %copy-done.3) | copy-start | bytes 6291460
  586.9 18.3 %copy-start.6 = (bf16[1024,1024]{1,0:T(8,128)(2,1)S(1)}, bf16[1024,1024]{1,0:T(8,128)(2,1)}, u32[]{:S(2)}) copy-start(bf16[1024,1024]{1,0:T(8,128)(2,1)} %copy-done.5) | copy-start | bytes 6291460
  588.9 16.5 %copy-start.2 = (bf16[1024,1024]{1,0:T(8,128)(2,1)S(1)}, bf16[1024,1024]{1,0:T(8,128)(2,1)}, u32[]{:S(2)}) copy-start(bf16[1024,1024]{1,0:T(8,128)(2,1)} %copy-done.1) | copy-start | bytes 6291460
  637.9 22.4 %copy-start.9 = (f32[2,512,64]{1,2,0:T(8,128)S(1)}, f32[2,512,64]{1,2,0:T(8,128)}, u32[]{:S(2)}) copy-start(f32[2,512,64]{1,2,0:T(8,128)} %copy-done.8) | copy-start | bytes 786436
  660.3 18.5 %copy-start.10 = (s32[2,16]{1,0:T(2,128)S(1)}, s32[2,16]{1,0:T(2,128)}, u32[]{:S(2)}) copy-start(s32[2,16]{1,0:T(2,128)} %param.13) | copy-start | bytes 388
Sparse Core Ops, SparseCore 0:
  8.9 49.5 all-gather.8
  60.4 156.0 all-gather.6
  218.1 46.8 all-gather.12
  266.5 57.1 all-gather.10
  325.1 73.0 all-gather.14
  399.7 237.5 all-gather.16
  867.8 204.5 reduce-scatter.1
